TPU v7x, 128 devices: a whole 4x4x4 slice. The times are simulated.
128 devices in a mesh: row: 4 (over x), col: 4 (over y_lo, core), layer: 8 (over y_hi, z).
Axes of the slice: x: 4, y: 4 (y_hi: 2, y_lo: 2; y = y_hi * 2 + y_lo), z: 4, core: 2. Of those that a mesh axis runs over, the one named last changes fastest.
Arguments:
- left_factor: float32 [6144, 8192], P('row', 'col'), may hold values from -6 to 6
- right_factor: float32 [8192, 6144], P('row', 'col'), may hold values from -0.0625 to 0.0625
Outputs:
- product: float32 [6144, 6144], P(('row', 'layer'), 'col')
All inputs are finite; a program needn't handle non-finite values.
Results may differ from a plain program's by a relative error of at most 0.000073.
Values sent between devices are 32-bit elements; how exact they have to be, the bound alone decides.
A program may use at most 192 MiB of HBM per device.

v0:
```python
import jax
import jax.numpy as jnp
from jax import lax
from jax.sharding import PartitionSpec as P

K = 8192
STEPS = 2


def broadcast(value, axis, root):
    mine = lax.axis_index(axis) == root
    return lax.psum(jnp.where(mine, value, jnp.zeros_like(value)), axis)


def per_device(left_factor, right_factor):
    block_depth = left_factor.shape[1]
    layers = lax.axis_size("layer")
    depth_index = lax.axis_index("layer")
    panel_width = K // (layers * STEPS)
    per_block = block_depth // panel_width
    group_size = 1
    gathered = []
    for step_index in range(0, STEPS, group_size):
        first_panel = depth_index * STEPS + step_index
        source = first_panel // per_block
        offset = first_panel % per_block * panel_width
        left_piece = lax.dynamic_slice_in_dim(left_factor, offset, group_size * panel_width, 1)
        right_piece = lax.dynamic_slice_in_dim(right_factor, offset, group_size * panel_width, 0)
        fetch_left_panel = broadcast(left_piece, "col", source)
        fetch_right_panel = broadcast(right_piece, "row", source)
        gathered.append((fetch_left_panel, fetch_right_panel))
    total = jnp.zeros((left_factor.shape[0], right_factor.shape[1]), jnp.float32)
    for left_panel, right_panel in gathered:
        total = total + jnp.dot(
            left_panel,
            right_panel,
            precision=lax.Precision.HIGHEST,
            preferred_element_type=jnp.float32,
        )
    return lax.psum_scatter(total, "layer", scatter_dimension=0, tiled=True)


def solution(mesh):
    placed = (P("row", "col"), P("row", "col"))
    return jax.shard_map(
        per_device,
        mesh=mesh,
        in_specs=placed,
        out_specs=P(("row", "layer"), "col"),
        check_vma=False,
    )
```

profile of v0, /device:TPU:0, one launch (start us, length us, event | category | flops | bytes accessed | tf_op | source)
XLA Modules:
  0.0 438.1 jit_solution(5593754253861912896)
XLA Ops:
  6.5 0.0 all-reduce.5.cloned.1.call-start
  6.5 6.3 %dynamic-slice_select_fusion.1 = (f32[1536,512]{1,0:T(8,128)}, f32[1536,512]{1,0:T(8,128)}) fusion(f32[1536,2048]{1,0:T(8,128)} %param.2, s32[]{:T(128)S(6)} %select_n.64, pred[]{:T(512)S(6)} %eq.17, s32[]{:T(128)S(6)} %select_n.57, pred[]{:T(512)S(6)} %eq.15), kind=kLoop, calls=%fused_computation.2 | loop fusion | flops 1572864 | bytes 12582922 | tf_op jit(solution)/shard_map/jit(_where)/select_n | solution.py:12
  12.8 0.0 all-reduce.5.cloned.1.call-update
  12.9 0.0 all-reduce.7.cloned.1.call-start
  12.9 6.1 %dynamic-slice_select_fusion = (f32[512,1536]{1,0:T(8,128)}, f32[512,1536]{1,0:T(8,128)}) fusion(f32[2048,1536]{1,0:T(8,128)} %param.3, s32[]{:T(128)S(6)} %select_n.64, pred[]{:T(512)S(6)} %eq.18, s32[]{:T(128)S(6)} %select_n.57, pred[]{:T(512)S(6)} %eq.16), kind=kLoop, calls=%fused_computation.1 | loop fusion | flops 1572864 | bytes 12582922 | tf_op jit(solution)/shard_map/jit(_where)/select_n | solution.py:12
  19.0 0.0 all-reduce.7.cloned.1.call-update
  19.1 0.0 reduce-scatter.2.cloned.1.call-start
  19.1 121.6 %all-reduce.5.cloned.1.call-done = (f32[1536,512]{1,0:T(8,128)}, f32[1536,512]{1,0:T(8,128)}) async-done(((f32[1536,512]{1,0:T(8,128)}, f32[1536,512]{1,0:T(8,128)}), (f32[1536,512]{1,0:T(8,128)}, f32[1536,512]{1,0:T(8,128)})) %all-reduce.5.cloned.1.call-update) | async-done | bytes 6291472 | tf_op jit(solution)/shard_map/psum | solution.py:12
  140.7 130.3 %all-reduce.7.cloned.1.call-done = (f32[512,1536]{1,0:T(8,128)}, f32[512,1536]{1,0:T(8,128)}) async-done(((f32[512,1536]{1,0:T(8,128)}, f32[512,1536]{1,0:T(8,128)}), (f32[512,1536]{1,0:T(8,128)}, f32[512,1536]{1,0:T(8,128)})) %all-reduce.7.cloned.1.call-update) | async-done | bytes 6291472 | tf_op jit(solution)/shard_map/psum | solution.py:12
  271.1 0.0 copy-start
  271.1 0.0 copy-start.1
  271.1 19.7 %fusion = f32[1536,1536]{1,0:T(8,128)S(1)} fusion(f32[1536,512]{1,0:T(8,128)} %get-tuple-element.5, f32[512,1536]{1,0:T(8,128)} %get-tuple-element.7), kind=kOutput, calls=%fused_computation.5 | convolution fusion | flops 14495514624 | bytes 15728640 | tf_op jit(solution)/shard_map/dot_general | solution.py:34
  290.8 0.0 copy-done
  290.8 0.0 copy-done.1
  290.8 18.6 %convolution_add_fusion = f32[1536,1536]{1,0:T(8,128)} fusion(f32[1536,1536]{1,0:T(8,128)S(1)} %fusion, f32[1536,512]{1,0:T(8,128)S(1)} %copy-done, f32[512,1536]{1,0:T(8,128)S(1)} %copy-done.1), kind=kOutput, calls=%fused_computation | convolution fusion | flops 14497873920 | bytes 25165824 | tf_op jit(solution)/shard_map/dot_general | solution.py:34
  309.3 0.0 reduce-scatter.2.cloned.1.call-update
  309.3 122.3 %reduce-scatter.2.cloned.1.call-done = f32[192,1536]{1,0:T(8,128)} async-done(((f32[1536,1536]{1,0:T(8,128)}), f32[192,1536]{1,0:T(8,128)}) %reduce-scatter.2.cloned.1.call-update) | async-done | bytes 1179664 | tf_op jit(solution)/shard_map/reduce_scatter | solution.py:40
Async XLA Ops:
  6.5 134.2 %all-reduce.5.cloned.1.call-start = ((), (), s32[]{:S(2)}) async-start(), calls=%async_computation.2 | async-start | bytes 12582912 | tf_op jit(solution)/shard_map/psum | solution.py:12
  12.9 258.2 %all-reduce.7.cloned.1.call-start = ((), (), s32[]{:S(2)}) async-start(), calls=%async_computation.3 | async-start | bytes 12582912 | tf_op jit(solution)/shard_map/psum | solution.py:12
  19.1 412.5 %reduce-scatter.2.cloned.1.call-start = ((), (), s32[]{:S(2)}) async-start(), calls=%async_computation.1 | async-start | bytes 10616832 | tf_op jit(solution)/shard_map/reduce_scatter | solution.py:40
  271.1 19.7 %copy-start = (f32[1536,512]{1,0:T(8,128)S(1)}, f32[1536,512]{1,0:T(8,128)}, u32[]{:S(2)}) copy-start(f32[1536,512]{1,0:T(8,128)} %get-tuple-element.6) | copy-start | bytes 9437188
  271.1 19.7 %copy-start.1 = (f32[512,1536]{1,0:T(8,128)S(1)}, f32[512,1536]{1,0:T(8,128)}, u32[]{:S(2)}) copy-start(f32[512,1536]{1,0:T(8,128)} %get-tuple-element.8) | copy-start | bytes 9437188
Sparse Core Ops, SparseCore 0:
  13.0 127.6 all-reduce.4
  143.1 127.9 all-reduce.6
  309.5 122.1 reduce-scatter.1
where the time goes:
time: 438 us
  waiting for transfers between devices  374 us (85%)
  matrix products  38.2 us (9%)
  between operations  13.1 us (3%)
  other arithmetic  12.4 us (3%)
    psum x2, waiting for transfers between devices, broadcast(): return lax.psum(jnp.where(mine, value, jnp.zeros_like(value)), axis)  252 us
    reduce_scatter x1, waiting for transfers between devices, per_device(): return lax.psum_scatter(total, 'layer', scatter_dimension=0, tiled=True)  122 us
    dot_general x2, matrix products, per_device(): jnp.dot(left_panel, right_panel, precision=lax.Precision.HIGHEST, preferr...  38.2 us
    select_n x2, other arithmetic, broadcast(): return lax.psum(jnp.where(mine, value, jnp.zeros_like(value)), axis)  12.4 us
  transfers between devices with their start and end apart: 3, of which 3 were waited for; matrix products, arithmetic and copies ran while one was open for 1% of the time, Pallas kernels for 0%

commit v1 on v0

v1 whole, which is shorter than its diff:
```python
import functools

import jax
import jax.numpy as jnp
from jax import lax
from jax.experimental import pallas as pl
from jax.experimental.pallas import tpu as pltpu
from jax.sharding import PartitionSpec as P

MESH = pl.DeviceIdType.MESH
RING = 4
WIDTHS = (256, 256, 256)


def split(x):
    high = x.astype(jnp.bfloat16)
    low = (x - high.astype(jnp.float32)).astype(jnp.bfloat16)
    return high, low


def kernel(
    a_hbm, b_hbm, out,
    a_buf, a_two, b_buf, b_high, b_low, part, hop_two, hop_one, final,
    a_local, a_core_s, a_core_r, a_y_s, a_y_r, a_relay_s, a_relay_r,
    b_local, b_s, b_r, b_relay_s, b_relay_r,
    two_s, two_r, one_s, one_r, swap_s, swap_r, keep,
):
    row, col, layer = lax.axis_index("row"), lax.axis_index("col"), lax.axis_index("layer")
    low_y, core = lax.div(col, 2), lax.rem(col, 2)
    high_y, z = lax.div(layer, RING), lax.rem(layer, RING)
    y = high_y * 2 + low_y

    def on_y(at):
        return (row, lax.rem(at, 2) * 2 + core, lax.div(at, 2) * RING + z)

    x_up = (lax.rem(row + 1, RING), col, layer)
    x_down = (lax.rem(row + RING - 1, RING), col, layer)
    y_up, y_down = on_y(lax.rem(y + 1, RING)), on_y(lax.rem(y + RING - 1, RING))
    z_up = (row, col, high_y * RING + lax.rem(z + 1, RING))
    z_down = (row, col, high_y * RING + lax.rem(z + RING - 1, RING))
    y_across = (row, col, (1 - high_y) * RING + z)
    twin = (row, low_y * 2 + 1 - core, layer)

    rows = part.shape[2]
    depth = b_buf.shape[0] // RING
    half_depth = depth // 2
    columns = b_buf.shape[1]
    chunks = []
    at = 0
    for width in WIDTHS:
        chunks.append((at, width))
        at += width
    assert at == columns

    def remote(src, dst, send, recv, device):
        return pltpu.make_async_remote_copy(
            src_ref=src, dst_ref=dst, send_sem=send, recv_sem=recv, device_id=device, device_id_type=MESH
        )

    def arrived(ref, send, recv):
        remote(ref, ref, send, recv, twin).wait_recv()

    sent = []

    def go(copy):
        copy.start()
        sent.append(copy)

    owners = [lax.rem(z + shift, RING) for shift in (2, 1, 3, 0)]
    k_at = pl.multiple_of(z * depth, depth)

    def a_source(step, half):
        first = pl.multiple_of(half * RING * rows + owners[step] * rows, rows)
        return a_hbm.at[pl.ds(first, rows), pl.ds(k_at, depth)]

    def a_place(step, half, quarter):
        return a_buf.at[step, half, :, pl.ds(pl.multiple_of(quarter * depth, depth), depth)]

    far_same = (1 - low_y) * 2 + core
    far_twin = (1 - low_y) * 2 + 1 - core
    near_twin = low_y * 2 + 1 - core

    def a_start(step):
        go(remote(a_source(step, 0), a_place(step, 0, col), a_y_s.at[step, 0], a_y_r.at[step, 0], y_up))
        go(remote(a_source(step, 1), a_place(step, 1, col), a_y_s.at[step, 1], a_y_r.at[step, 1], y_down))
        for half in range(2):
            pltpu.make_async_copy(a_source(step, half), a_place(step, half, col), a_local.at[step, half]).start()
            go(remote(a_source(step, half), a_place(step, half, col), a_core_s.at[step, half], a_core_r.at[step, half], twin))

    def a_relay(step):
        for half in range(2):
            here = a_place(step, half, far_same)
            arrived(here, a_y_s.at[step, half], a_y_r.at[step, half])
            go(remote(here, here, a_relay_s.at[step, half], a_relay_r.at[step, half], twin))

    def a_split(step):
        for half in range(2):
            pltpu.make_async_copy(a_source(step, half), a_place(step, half, col), a_local.at[step, half]).wait()
            arrived(a_place(step, half, near_twin), a_core_s.at[step, half], a_core_r.at[step, half])
            arrived(a_place(step, half, far_twin), a_relay_s.at[step, half], a_relay_r.at[step, half])

            @pl.loop(0, rows // 16)
            def _(tile):
                band = pl.ds(pl.multiple_of(tile * 16, 16), 16)
                high, low = split(a_buf[step, half, band, :])
                a_two[step, half, 0, band, :] = high
                a_two[step, half, 1, band, :] = low

    def b_source(chunk, part_of):
        first, width = chunks[chunk]
        return b_hbm.at[
            pl.ds(pl.multiple_of(z * depth + part_of * half_depth, half_depth), half_depth),
            pl.ds(pl.multiple_of(high_y * columns + first, 128), width),
        ]

    def b_place(chunk, part_of, quarter):
        first, width = chunks[chunk]
        return b_buf.at[
            pl.ds(pl.multiple_of(quarter * depth + part_of * half_depth, half_depth), half_depth), pl.ds(first, width)
        ]

    row_up, row_down = x_up[0], x_down[0]
    row_across = lax.rem(row + 2, RING)

    def b_keep(chunk):
        for part_of in range(2):
            pltpu.make_async_copy(
                b_source(chunk, part_of), b_place(chunk, part_of, row), b_local.at[chunk, part_of]
            ).start()

    def b_start(chunk):
        for turn in range(2):
            up, down = turn, 1 - turn
            go(remote(b_source(chunk, up), b_place(chunk, up, row), b_s.at[chunk, 0, up], b_r.at[chunk, 0, up], x_up))
            go(remote(b_source(chunk, down), b_place(chunk, down, row), b_s.at[chunk, 1, down], b_r.at[chunk, 1, down], x_down))

    def b_relay(chunk):
        here = b_place(chunk, 0, row_down)
        arrived(here, b_s.at[chunk, 0, 0], b_r.at[chunk, 0, 0])
        go(remote(here, here, b_relay_s.at[chunk, 0], b_relay_r.at[chunk, 0], x_up))
        here = b_place(chunk, 1, row_up)
        arrived(here, b_s.at[chunk, 1, 1], b_r.at[chunk, 1, 1])
        go(remote(here, here, b_relay_s.at[chunk, 1], b_relay_r.at[chunk, 1], x_down))

    def b_split(chunk):
        for part_of in range(2):
            pltpu.make_async_copy(
                b_source(chunk, part_of), b_place(chunk, part_of, row), b_local.at[chunk, part_of]
            ).wait()
            arrived(b_place(chunk, part_of, row_across), b_relay_s.at[chunk, part_of], b_relay_r.at[chunk, part_of])
        arrived(b_place(chunk, 1, row_down), b_s.at[chunk, 0, 1], b_r.at[chunk, 0, 1])
        arrived(b_place(chunk, 0, row_up), b_s.at[chunk, 1, 0], b_r.at[chunk, 1, 0])
        first, width = chunks[chunk]
        cols = pl.ds(first, width)

        @pl.loop(0, b_buf.shape[0] // 64)
        def _(tile):
            band = pl.ds(pl.multiple_of(tile * 64, 64), 64)
            high, low = split(b_buf[band, cols])
            b_high[band, cols] = high
            b_low[band, cols] = low

    def c_cols(chunk):
        first, width = chunks[chunk]
        return pl.ds(first, width)

    def multiply(chunk, step):
        cols = c_cols(chunk)

        @pl.loop(0, 2)
        def _(half):
            both = a_two[step, half].reshape(2 * rows, -1)
            by_high = jnp.dot(both, b_high[:, cols], preferred_element_type=jnp.float32)
            by_low = jnp.dot(a_two[step, half, 0], b_low[:, cols], preferred_element_type=jnp.float32)
            part[step, half, :, cols] = by_high[:rows] + (by_high[rows:] + by_low)

        if step == 0:
            go(remote(part.at[0, 0, :, cols], hop_two.at[0, :, cols], two_s.at[chunk, 0], two_r.at[chunk, 0], z_up))
            go(remote(part.at[0, 1, :, cols], hop_two.at[1, :, cols], two_s.at[chunk, 1], two_r.at[chunk, 1], z_down))
        if step == 1:
            c_send(chunk, 1, 1)
        if step == 2:
            c_send(chunk, 2, 0)

    def c_send(chunk, step, half):
        cols = c_cols(chunk)
        way, device = (0, z_up) if step == 1 else (1, z_down)
        go(remote(part.at[step, half, :, cols], hop_one.at[way, half, :, cols], one_s.at[chunk, way, half], one_r.at[chunk, way, half], device))

    def add(chunk, step):
        cols = c_cols(chunk)
        half = step - 1
        arrived(hop_two.at[half, :, cols], two_s.at[chunk, half], two_r.at[chunk, half])
        part[step, half, :, cols] += hop_two[half, :, cols]
        c_send(chunk, step, half)

    def out_cols(chunk, side):
        first, width = chunks[chunk]
        return out.at[:, pl.ds(pl.multiple_of(side * columns + first, 128), width)]

    def finish(chunk):
        cols = c_cols(chunk)
        for half in (1, 0):
            for way in range(2):
                arrived(hop_one.at[way, half, :, cols], one_s.at[chunk, way, half], one_r.at[chunk, way, half])
            final[half, :, cols] = part[3, half, :, cols] + hop_one[0, half, :, cols] + hop_one[1, half, :, cols]
        go(remote(final.at[1 - high_y, :, cols], out_cols(chunk, high_y), swap_s.at[chunk], swap_r.at[chunk], y_across))
        pltpu.make_async_copy(final.at[high_y, :, cols], out_cols(chunk, high_y), keep.at[chunk]).start()

    barrier = pltpu.get_barrier_semaphore()
    peers = (x_up, x_down, y_up, y_down, z_up, z_down, y_across, twin)
    for peer in peers:
        pl.semaphore_signal(barrier, inc=1, device_id=peer, device_id_type=MESH)
    pl.semaphore_wait(barrier, len(peers))

    b_start(0)
    for step in range(4):
        a_start(step)
    for chunk in range(len(chunks)):
        b_keep(chunk)

    b_relay(0)
    b_start(1)
    a_relay(0)
    a_split(0)
    a_relay(1)
    b_split(0)
    multiply(0, 0)
    a_split(1)
    multiply(0, 1)
    b_relay(1)
    b_start(2)
    add(0, 1)
    a_relay(2)
    a_split(2)
    multiply(0, 2)
    add(0, 2)
    a_relay(3)
    a_split(3)
    multiply(0, 3)
    b_split(1)
    multiply(1, 0)
    multiply(1, 1)
    multiply(1, 2)
    b_relay(2)
    add(1, 1)
    add(1, 2)
    finish(0)
    multiply(1, 3)
    finish(1)
    b_split(2)
    for step in range(4):
        multiply(2, step)
    add(2, 1)
    add(2, 2)
    finish(2)

    for copy in sent:
        copy.wait_send()
    for chunk in range(len(chunks)):
        arrived(out_cols(chunk, 1 - high_y), swap_s.at[chunk], swap_r.at[chunk])
        pltpu.make_async_copy(final.at[high_y, :, c_cols(chunk)], out_cols(chunk, high_y), keep.at[chunk]).wait()


def per_device(left_factor, right_factor):
    layers = lax.axis_size("layer")
    rows = left_factor.shape[0] // layers
    depth = left_factor.shape[1] // RING
    full_depth = left_factor.shape[1]
    columns = right_factor.shape[1] // 2
    count = len(WIDTHS)
    dma = pltpu.SemaphoreType.DMA
    f32, bf16 = jnp.float32, jnp.bfloat16
    return pl.pallas_call(
        kernel,
        out_shape=jax.ShapeDtypeStruct((rows, 2 * columns), f32),
        in_specs=[pl.BlockSpec(memory_space=pl.ANY)] * 2,
        out_specs=pl.BlockSpec(memory_space=pl.ANY),
        scratch_shapes=[
            pltpu.VMEM((4, 2, rows, full_depth), f32),
            pltpu.VMEM((4, 2, 2, rows, full_depth), bf16),
            pltpu.VMEM((full_depth, columns), f32),
            pltpu.VMEM((full_depth, columns), bf16),
            pltpu.VMEM((full_depth, columns), bf16),
            pltpu.VMEM((4, 2, rows, columns), f32),
            pltpu.VMEM((2, rows, columns), f32),
            pltpu.VMEM((2, 2, rows, columns), f32),
            pltpu.VMEM((2, rows, columns), f32),
            dma((4, 2)), dma((4, 2)), dma((4, 2)), dma((4, 2)), dma((4, 2)), dma((4, 2)), dma((4, 2)),
            dma((count, 2)), dma((count, 2, 2)), dma((count, 2, 2)), dma((count, 2)), dma((count, 2)),
            dma((count, 2)), dma((count, 2)), dma((count, 2, 2)), dma((count, 2, 2)),
            dma((count,)), dma((count,)), dma((count,)),
        ],
        compiler_params=pltpu.CompilerParams(
            collective_id=0, has_side_effects=True, vmem_limit_bytes=64000 * 1024
        ),
        name="product",
    )(left_factor, right_factor)


def solution(mesh):
    placed = (P("row", "col"), P("row", "col"))
    return jax.shard_map(
        per_device,
        mesh=mesh,
        in_specs=placed,
        out_specs=P(("row", "layer"), "col"),
        check_vma=False,
    )
```

time: 438 us -> 88.9 us (0.20)
  waiting for transfers between devices: 374 us -> 0 us
  Pallas kernels: 0 us -> 86.4 us
  matrix products: 38.2 us -> 0 us
  between operations: 13.1 us -> 0.01 us
  other arithmetic: 12.4 us -> 0 us
    psum x2 -> x0, waiting for transfers between devices: 252 us -> none  [broadcast(): return lax.psum(jnp.where(mine, value, jnp.zeros_like(value)), axis)]
    reduce_scatter x1 -> x0, waiting for transfers between devices: 122 us -> none  [per_device(): return lax.psum_scatter(total, 'layer', scatter_dimension=0, tiled=True)]
    pallas_call x0 -> x1, Pallas kernels: none -> 86.4 us  [per_device(): pl.pallas_call(kernel, out_shape=jax.ShapeDtypeStruct((rows, 2 * columns)...]
    dot_general x2 -> x0, matrix products: 38.2 us -> none  [per_device(): jnp.dot(left_panel, right_panel, precision=lax.Precision.HIGHEST, preferr...]
    select_n x2 -> x0, other arithmetic: 12.4 us -> none  [broadcast(): return lax.psum(jnp.where(mine, value, jnp.zeros_like(value)), axis)]
  transfers between devices with their start and end apart: 3 -> 0, of which waited for: 3 -> 0; matrix products, arithmetic and copies ran while one was open for 1% -> 0% of each run, Pallas kernels for 0% -> 0%
where the time goes in v1:
time: 88.9 us; the launch traced here: 88.8 us
  Pallas kernels  86.4 us (97%)
  local copies, waits for them, and re-layouts  2.36 us (3%)
    pallas_call x1, Pallas kernels, per_device(): pl.pallas_call(kernel, out_shape=jax.ShapeDtypeStruct((rows, 2 * columns)...  86.4 us
    unnamed x1, local copies, waits for them, and re-layouts  2.36 us

profile of v1, /device:TPU:0, one launch (start us, length us, event | category | flops | bytes accessed | tf_op | source)
XLA Modules:
  0.0 88.8 jit_solution(10577884895231890515)
XLA Ops:
  0.0 86.4 %product.1 = f32[192,1536]{1,0:T(8,128)} custom-call(f32[1536,2048]{1,0:T(8,128)} %a_hbm.1, f32[2048,1536]{1,0:T(8,128)} %b_hbm.1), custom_call_target="tpu_custom_call" | custom-call | tf_op jit(solution)/shard_map/product/pallas_call | solution.py:274
  86.4 2.4 %copy.4 = f32[192,1536]{1,0:T(8,128)} copy(f32[192,1536]{1,0:T(8,128)} %product.1) | data formatting | bytes 2359296
